TPU v7x, 256 devices: a whole 4x4x8 slice. The times are simulated.
256 devices in a mesh: dp: 8 (over z), vocab: 32 (over x, y, core).
Axes of the slice: x: 4, y: 4, z: 8, core: 2. Of those that a mesh axis runs over, the one named last changes fastest.
Arguments:
- token_ids: int32 [65536], P(('dp', 'vocab')), may hold values from 0 to 152063, as said below
- token_count: int32 [256], P(('dp', 'vocab')), may hold values from 16 to 256
- out_grads: bfloat16 [65536, 5120], P(('dp', 'vocab')), may hold values from -18 to 18
- master_rows: float32 [16384, 5120], P('vocab', 'dp'), may hold values from -0.8 to 0.8
- first_moment: float32 [16384, 5120], P('vocab', 'dp'), may hold values from -4 to 4
- second_moment: float32 [16384, 5120], P('vocab', 'dp'), may hold values from 0.001 to 1
Outputs:
- new_master: float32 [16384, 5120], P('vocab', 'dp')
- new_first: float32 [16384, 5120], P('vocab', 'dp')
- new_second: float32 [16384, 5120], P('vocab', 'dp')
- table_rows: bfloat16 [16384, 5120], P('vocab')
Inputs may be any that keep to these rules, and one draw needn't show every extreme that they name: `token_ids`: within each block of 256 slots, among the live slots (the first token_count of the block) at most 8 have ids in the new rows j * 512 + 135680 to (j + 1) * 512 + 135679 for any one j, and for some j exactly 8 in every block. Slots past token_count hold ids of new rows that are to be ignored.
All inputs are finite; a program needn't handle non-finite values.
Results may differ from a plain program's by a relative error of at most 0.001.
Values may be sent and summed in bfloat16 or wider, within the bound.
No kernel may reach another device: no remote copies, remote signals or barrier semaphores. Data moves between devices by JAX's collectives and lax.ppermute only.
A program may use at most 64 MiB of HBM per device.

v0:
```python
import jax
import jax.numpy as jnp
from jax import lax
from jax.sharding import PartitionSpec as P

VOCAB = 152064
CAP = 8
beta_one = 0.9
beta_two = 0.999
corr_one = 1.0 - 0.9**10
corr_two = 1.0 - 0.999**10
learn_rate = 0.01
epsilon = 1e-08


def body(token_ids, token_count, out_grads, master_rows, first_moment, second_moment):
    owners = lax.axis_size("vocab")
    groups = lax.axis_size("dp")
    rows_own = master_rows.shape[0]
    tok_slots = token_ids.shape[0]
    first_new = VOCAB - rows_own * owners
    position = jnp.arange(tok_slots)
    is_live = (position < token_count[0]) & (token_ids >= first_new)
    new_index = token_ids - first_new
    owner_of = new_index // rows_own
    row_in_owner = new_index % rows_own
    belongs = (owner_of[:, None] == jnp.arange(owners)[None, :]) & is_live[:, None]
    ranking = jnp.cumsum(belongs.astype(jnp.int32), axis=0) - 1
    my_rank = jnp.sum(jnp.where(belongs, ranking, 0), axis=1)
    slot_index = jnp.where(is_live, owner_of * CAP + my_rank, -1)
    placing = jnp.arange(owners * CAP)[:, None] == slot_index[None, :]
    outgoing = jnp.dot(
        placing.astype(jnp.bfloat16), out_grads, preferred_element_type=jnp.float32
    ).astype(jnp.bfloat16)
    slot_row = jnp.max(jnp.where(placing, row_in_owner[None, :], -1), axis=1)
    upper_part = jnp.where(slot_row >= 0, slot_row // 16, -1)
    lower_part = jnp.where(slot_row >= 0, slot_row % 16, 0)
    row_pairs = jnp.stack([upper_part, lower_part], axis=1).astype(jnp.bfloat16)
    tiled_pairs = jnp.tile(row_pairs, (1, groups))
    split_grads, split_pairs = (
        lax.all_to_all(outgoing, "dp", split_axis=1, concat_axis=0, tiled=True),
        lax.all_to_all(tiled_pairs, "dp", split_axis=1, concat_axis=0, tiled=True),
    )
    split_grads = split_grads.reshape(groups, owners * CAP, split_grads.shape[1])
    split_pairs = split_pairs.reshape(groups, owners * CAP, 2)
    arrived, arrived_pairs = (
        lax.all_to_all(split_grads, "vocab", split_axis=1, concat_axis=0, tiled=True),
        lax.all_to_all(split_pairs, "vocab", split_axis=1, concat_axis=0, tiled=True),
    )
    arrived = arrived.reshape(-1, arrived.shape[2])
    arrived_pairs = arrived_pairs.reshape(-1, 2).astype(jnp.float32)
    decoded = arrived_pairs[:, 0] * 16.0 + arrived_pairs[:, 1]
    selector = decoded[None, :] == jnp.arange(rows_own, dtype=jnp.float32)[:, None]
    gradient = jnp.dot(selector.astype(jnp.bfloat16), arrived, preferred_element_type=jnp.float32)
    new_first = beta_one * first_moment + (1.0 - beta_one) * gradient
    new_second = beta_two * second_moment + (1.0 - beta_two) * gradient * gradient
    update = new_first / corr_one / (jnp.sqrt(new_second / corr_two) + epsilon)
    new_master = master_rows - learn_rate * update
    table_rows = lax.all_gather(new_master.astype(jnp.bfloat16), "dp", axis=1, tiled=True)
    return (new_master, new_first, new_second, table_rows)


def solution(mesh):
    return jax.shard_map(
        body,
        mesh=mesh,
        in_specs=(
            P(("dp", "vocab")),
            P(("dp", "vocab")),
            P(("dp", "vocab"), None),
            P("vocab", "dp"),
            P("vocab", "dp"),
            P("vocab", "dp"),
        ),
        out_specs=(P("vocab", "dp"), P("vocab", "dp"), P("vocab", "dp"), P("vocab", None)),
        check_vma=False,
    )
```

profile of v0, /device:TPU:1, one launch (start us, length us, event | category | flops | bytes accessed | tf_op | source)
XLA Modules:
  0.0 226.1 jit_solution(13173120727746846813)
XLA Ops:
  7.2 0.0 copy-start
  8.0 0.7 and_select_fusion.2
  8.7 0.7 fusion.15
  9.4 0.7 compare_and_fusion
  10.0 0.6 reduce-window.6
  10.6 0.2 slice_reduce_fusion
  10.9 0.1 fusion.5
  11.0 0.7 add_select_fusion
  11.7 0.1 select_reduce_fusion
  11.8 0.6 tile.2
  12.4 9.0 %all-to-all-start = ((bf16[256,8,2]{0,2,1:T(2,128)(2,1)}), bf16[256,8,2]{0,2,1:T(2,128)(2,1)S(1)}, u32[]{:S(2)}, u32[]{:S(2)}) async-start(bf16[256,8,2]{0,2,1:T(2,128)(2,1)} %tile.2), calls=%async_computation | async-start | bytes 16384 | tf_op jit(solution)/shard_map/all_to_all | solution.py:42
  21.4 0.0 copy-done
  21.4 0.8 convolution_convert_fusion
  22.3 1.7 copy.51
  24.0 4.0 %all-to-all-done = bf16[256,8,2]{0,2,1:T(2,128)(2,1)S(1)} async-done(((bf16[256,8,2]{0,2,1:T(2,128)(2,1)}), bf16[256,8,2]{0,2,1:T(2,128)(2,1)S(1)}, u32[]{:S(2)}, u32[]{:S(2)}) %all-to-all-start) | async-done | bytes 8224 | tf_op jit(solution)/shard_map/all_to_all | solution.py:42
  28.0 4.4 %all-to-all-start.2 = ((bf16[256,8,640]{2,0,1:T(8,128)(2,1)}), bf16[256,8,640]{2,0,1:T(8,128)(2,1)}, u32[]{:S(2)}, u32[]{:S(2)}) async-start(bf16[256,8,640]{2,0,1:T(8,128)(2,1)} %bitcast.43), calls=%async_computation.2 | async-start | bytes 5242880 | tf_op jit(solution)/shard_map/all_to_all | solution.py:41
  32.4 0.8 copy.39
  33.2 58.8 %all-to-all-done.2 = bf16[256,8,640]{2,0,1:T(8,128)(2,1)} async-done(((bf16[256,8,640]{2,0,1:T(8,128)(2,1)}), bf16[256,8,640]{2,0,1:T(8,128)(2,1)}, u32[]{:S(2)}, u32[]{:S(2)}) %all-to-all-start.2) | async-done | bytes 2621472 | tf_op jit(solution)/shard_map/all_to_all | solution.py:41
  92.0 10.9 %all-to-all-start.1 = ((bf16[8,256,2]{0,2,1:T(2,128)(2,1)}), bf16[8,256,2]{0,2,1:T(2,128)(2,1)S(1)}, u32[]{:S(2)}, u32[]{:S(2)}) async-start(bf16[8,256,2]{0,2,1:T(2,128)(2,1)} %copy.39), calls=%async_computation.1 | async-start | bytes 262144 | tf_op jit(solution)/shard_map/all_to_all | solution.py:48
  103.0 4.7 %copy.43 = bf16[8,256,640]{2,0,1:T(8,128)(2,1)} copy(bf16[8,256,640]{2,1,0:T(8,128)(2,1)} %bitcast.8) | data formatting | bytes 5242880 | tf_op jit(solution)/shard_map/all_to_all | solution.py:41
  107.7 2.9 %all-to-all-done.1 = bf16[8,256,2]{0,2,1:T(2,128)(2,1)S(1)} async-done(((bf16[8,256,2]{0,2,1:T(2,128)(2,1)}), bf16[8,256,2]{0,2,1:T(2,128)(2,1)S(1)}, u32[]{:S(2)}, u32[]{:S(2)}) %all-to-all-start.1) | async-done | bytes 8224 | tf_op jit(solution)/shard_map/all_to_all | solution.py:48
  110.7 4.8 %all-to-all-start.3 = ((bf16[8,256,640]{2,0,1:T(8,128)(2,1)}), bf16[8,256,640]{2,0,1:T(8,128)(2,1)}, u32[]{:S(2)}, u32[]{:S(2)}) async-start(bf16[8,256,640]{2,0,1:T(8,128)(2,1)} %copy.43), calls=%async_computation.3 | async-start | bytes 5242880 | tf_op jit(solution)/shard_map/all_to_all | solution.py:47
  115.4 0.0 all-gather.2.cloned.1.call-start
  115.5 0.1 copy.40
  115.6 0.2 reshape.169
  115.8 0.2 copy.41
  115.9 0.2 reshape.168
  116.1 33.4 %all-to-all-done.3 = bf16[8,256,640]{2,0,1:T(8,128)(2,1)} async-done(((bf16[8,256,640]{2,0,1:T(8,128)(2,1)}), bf16[8,256,640]{2,0,1:T(8,128)(2,1)}, u32[]{:S(2)}, u32[]{:S(2)}) %all-to-all-start.3) | async-done | bytes 2621472 | tf_op jit(solution)/shard_map/all_to_all | solution.py:47
  149.5 0.0 copy-start.1
  149.5 0.0 copy-start.2
  149.5 0.0 copy-start.3
  149.5 2.4 %copy.45 = bf16[32,8,8,640]{3,2,1,0:T(8,128)(2,1)S(1)} copy(bf16[32,8,8,640]{3,1,2,0:T(8,128)(2,1)} %bitcast.11) | data formatting | bytes 5242880 | tf_op jit(solution)/shard_map/all_to_all | solution.py:47
  151.9 0.0 copy-done.1
  151.9 0.1 copy-done.2
  152.0 0.4 copy-done.3
  152.4 4.7 %fusion.11 = (bf16[512,640]{1,0:T(8,128)(2,1)}, f32[512,640]{1,0:T(8,128)}, f32[512,640]{1,0:T(8,128)}, f32[512,640]{1,0:T(8,128)}) fusion(f32[512,640]{1,0:T(8,128)S(1)} %copy-done.1, f32[512,640]{1,0:T(8,128)S(1)} %copy-done.2, f32[512,640]{1,0:T(8,128)S(1)} %copy-done.3, bf16[2048,640]{1,0:T(8,128)(2,1)S(1)} %bitcast.45, f32[2048]{0:T(1024)S(1)} %bitcast.49), kind=kOutput, calls=%fused_computation.43 | convolution fusion | flops 1347813376 | bytes 11149312 | tf_op jit(solution)/shard_map/dot_general | solution.py:54
  157.1 0.0 all-gather.2.cloned.1.call-update
  157.1 57.0 %all-gather.2.cloned.1.call-done = bf16[512,5120]{1,0:T(8,128)(2,1)} async-done(((bf16[512,640]{1,0:T(8,128)(2,1)}), bf16[512,5120]{1,0:T(8,128)(2,1)}) %all-gather.2.cloned.1.call-update) | async-done | bytes 5242896 | tf_op jit(solution)/shard_map/all_gather | solution.py:59
  214.1 5.2 %copy.54 = bf16[512,5120]{1,0:T(8,128)(2,1)} copy(bf16[512,5120]{1,0:T(8,128)(2,1)} %all-gather.2.cloned.1.call-done) | data formatting | bytes 10485760
  (6 shorter events, 0.1 us)
Async XLA Ops:
  7.2 14.3 %copy-start = (bf16[256,5120]{1,0:T(8,128)(2,1)S(1)}, bf16[256,5120]{1,0:T(8,128)(2,1)}, u32[]{:S(2)}) copy-start(bf16[256,5120]{1,0:T(8,128)(2,1)} %param.8) | copy-start | bytes 7864324
  12.4 15.6 %all-to-all-start = ((bf16[256,8,2]{0,2,1:T(2,128)(2,1)}), bf16[256,8,2]{0,2,1:T(2,128)(2,1)S(1)}, u32[]{:S(2)}, u32[]{:S(2)}) async-start(bf16[256,8,2]{0,2,1:T(2,128)(2,1)} %tile.2), calls=%async_computation | async-start | bytes 16384 | tf_op jit(solution)/shard_map/all_to_all | solution.py:42
  28.0 64.0 %all-to-all-start.2 = ((bf16[256,8,640]{2,0,1:T(8,128)(2,1)}), bf16[256,8,640]{2,0,1:T(8,128)(2,1)}, u32[]{:S(2)}, u32[]{:S(2)}) async-start(bf16[256,8,640]{2,0,1:T(8,128)(2,1)} %bitcast.43), calls=%async_computation.2 | async-start | bytes 5242880 | tf_op jit(solution)/shard_map/all_to_all | solution.py:41
  92.0 18.6 %all-to-all-start.1 = ((bf16[8,256,2]{0,2,1:T(2,128)(2,1)}), bf16[8,256,2]{0,2,1:T(2,128)(2,1)S(1)}, u32[]{:S(2)}, u32[]{:S(2)}) async-start(bf16[8,256,2]{0,2,1:T(2,128)(2,1)} %copy.39), calls=%async_computation.1 | async-start | bytes 262144 | tf_op jit(solution)/shard_map/all_to_all | solution.py:48
  110.7 38.9 %all-to-all-start.3 = ((bf16[8,256,640]{2,0,1:T(8,128)(2,1)}), bf16[8,256,640]{2,0,1:T(8,128)(2,1)}, u32[]{:S(2)}, u32[]{:S(2)}) async-start(bf16[8,256,640]{2,0,1:T(8,128)(2,1)} %copy.43), calls=%async_computation.3 | async-start | bytes 5242880 | tf_op jit(solution)/shard_map/all_to_all | solution.py:47
  115.4 98.7 %all-gather.2.cloned.1.call-start = ((), (), s32[]{:S(2)}) async-start(), calls=%async_computation.4 | async-start | bytes 5898240 | tf_op jit(solution)/shard_map/all_gather | solution.py:59
  149.5 2.4 %copy-start.1 = (f32[512,640]{1,0:T(8,128)S(1)}, f32[512,640]{1,0:T(8,128)}, u32[]{:S(2)}) copy-start(f32[512,640]{1,0:T(8,128)} %param.9) | copy-start | bytes 3932164
  149.5 2.5 %copy-start.2 = (f32[512,640]{1,0:T(8,128)S(1)}, f32[512,640]{1,0:T(8,128)}, u32[]{:S(2)}) copy-start(f32[512,640]{1,0:T(8,128)} %param.10) | copy-start | bytes 3932164
  149.5 2.9 %copy-start.3 = (f32[512,640]{1,0:T(8,128)S(1)}, f32[512,640]{1,0:T(8,128)}, u32[]{:S(2)}) copy-start(f32[512,640]{1,0:T(8,128)} %param.11) | copy-start | bytes 3932164
Sparse Core Ops, SparseCore 0:
  157.2 56.8 all-gather.1
where the time goes:
time: 227 us; the launch traced here: 226 us
  waiting for transfers between devices  156 us (69%)
  starting transfers between devices  29.2 us (13%)
  local copies, waits for them, and re-layouts  16.7 us (7%)
  between operations  14.9 us (7%)
  matrix products  5.52 us (2%)
  other arithmetic  3.65 us (2%)
    all_to_all x1, waiting for transfers between devices, body(): lax.all_to_all(outgoing, 'dp', split_axis=1, concat_axis=0, tiled=True)  58.8 us
    all_gather x1, waiting for transfers between devices, body(): lax.all_gather(new_master.astype(jnp.bfloat16), 'dp', axis=1, tiled=True)  57 us
    all_to_all x1, waiting for transfers between devices, body(): lax.all_to_all(split_grads, 'vocab', split_axis=1, concat_axis=0, tiled=T...  33.4 us
    all_to_all x1, starting transfers between devices, body(): lax.all_to_all(split_pairs, 'vocab', split_axis=1, concat_axis=0, tiled=T...  10.9 us
    all_to_all x1, starting transfers between devices, body(): lax.all_to_all(tiled_pairs, 'dp', split_axis=1, concat_axis=0, tiled=True)  9 us
    all_to_all x2, local copies, waits for them, and re-layouts, body(): lax.all_to_all(outgoing, 'dp', split_axis=1, concat_axis=0, tiled=True)  6.47 us
    unnamed x9, local copies, waits for them, and re-layouts  5.69 us
    all_to_all x1, starting transfers between devices, body(): lax.all_to_all(split_grads, 'vocab', split_axis=1, concat_axis=0, tiled=T...  4.79 us
  transfers between devices with their start and end apart: 5, of which 5 were waited for; matrix products, arithmetic and copies ran while one was open for 4% of the time, Pallas kernels for 0%

commit v1 on v0

--- a/solution.py
+++ b/solution.py
@@ -11,6 +11,29 @@
 corr_two = 1.0 - 0.999**10
 learn_rate = 0.01
 epsilon = 1e-08
+
+
+def cut_along(x, dim, count):
+    lengths = x.shape
+    blocks = x.reshape(*lengths[:dim], count, lengths[dim] // count, *lengths[dim + 1 :])
+    return jnp.moveaxis(blocks, dim, 0)
+
+
+def joined_along(parts, dim):
+    parts = jnp.moveaxis(parts, 0, dim)
+    shape = parts.shape
+    return parts.reshape(*shape[:dim], shape[dim] * shape[dim + 1], *shape[dim + 2 :])
+
+
+def sent_to_each(x, axis, split_dim, concat_dim):
+    size, index = (lax.axis_size(axis), lax.axis_index(axis))
+    tiles = cut_along(x, split_dim, size)
+    done = [tiles[index]]
+    for lap in range(1, size):
+        sent = tiles[(index + lap) % size]
+        done.append(lax.ppermute(sent, axis, [(i, (i + lap) % size) for i in range(size)]))
+    tiles = jnp.stack(done)[(index - jnp.arange(size)) % size]
+    return joined_along(tiles, concat_dim)
 
 
 def body(token_ids, token_count, out_grads, master_rows, first_moment, second_moment):
@@ -38,7 +61,7 @@
     row_pairs = jnp.stack([upper_part, lower_part], axis=1).astype(jnp.bfloat16)
     tiled_pairs = jnp.tile(row_pairs, (1, groups))
     split_grads, split_pairs = (
-        lax.all_to_all(outgoing, "dp", split_axis=1, concat_axis=0, tiled=True),
+        sent_to_each(outgoing, "dp", 1, 0),
         lax.all_to_all(tiled_pairs, "dp", split_axis=1, concat_axis=0, tiled=True),
     )
     split_grads = split_grads.reshape(groups, owners * CAP, split_grads.shape[1])

time: 227 us -> 239 us (1.053)
  waiting for transfers between devices: 156 us -> 122 us
  local copies, waits for them, and re-layouts: 16.7 us -> 50 us
  starting transfers between devices: 29.2 us -> 42.3 us
    all_to_all x1 -> x0, waiting for transfers between devices: 58.8 us -> none  [body(): lax.all_to_all(outgoing, 'dp', split_axis=1, concat_axis=0, tiled=True)]
    ppermute x0 -> x7, waiting for transfers between devices: none -> 29.8 us  [sent_to_each(): lax.ppermute(sent, axis, [(i, (i + lap) % size) for i in range(size)])]
    unnamed x9 -> x24, local copies, waits for them, and re-layouts: 5.69 us -> 21.3 us
    another operation x1 -> x3, local copies, waits for them, and re-layouts: 0.01 us -> 15.4 us
    ppermute x0 -> x7, starting transfers between devices: none -> 15 us  [sent_to_each(): lax.ppermute(sent, axis, [(i, (i + lap) % size) for i in range(size)])]
    gather x0 -> x2, local copies, waits for them, and re-layouts: none -> 8.84 us  [sent_to_each(): tiles = jnp.stack(done)[(index - jnp.arange(size)) % size]]
    all_to_all x2 -> x0, local copies, waits for them, and re-layouts: 6.47 us -> none  [body(): lax.all_to_all(outgoing, 'dp', split_axis=1, concat_axis=0, tiled=True)]
    all_to_all x1 -> x0, starting transfers between devices: 4.39 us -> none  [body(): lax.all_to_all(outgoing, 'dp', split_axis=1, concat_axis=0, tiled=True)]
  transfers between devices with their start and end apart: 5 -> 11, of which waited for: 5 -> 6; matrix products, arithmetic and copies ran while one was open for 4% -> 18% of each run, Pallas kernels for 0% -> 0%
where the time goes in v1:
time: 239 us
  waiting for transfers between devices  122 us (51%)
  local copies, waits for them, and re-layouts  50 us (21%)
  starting transfers between devices  42.3 us (18%)
  between operations  15 us (6%)
  matrix products  5.52 us (2%)
  other arithmetic  3.66 us (2%)
    all_gather x1, waiting for transfers between devices, body(): lax.all_gather(new_master.astype(jnp.bfloat16), 'dp', axis=1, tiled=True)  59.3 us
    all_to_all x1, waiting for transfers between devices, body(): lax.all_to_all(split_grads, 'vocab', split_axis=1, concat_axis=0, tiled=T...  33.3 us
    ppermute x7, waiting for transfers between devices, sent_to_each(): lax.ppermute(sent, axis, [(i, (i + lap) % size) for i in range(size)])  29.8 us
    unnamed x24, local copies, waits for them, and re-layouts  21.3 us
    ppermute x7, starting transfers between devices, sent_to_each(): lax.ppermute(sent, axis, [(i, (i + lap) % size) for i in range(size)])  15 us
    another operation x2, local copies, waits for them, and re-layouts  14.6 us
    all_to_all x1, starting transfers between devices, body(): lax.all_to_all(split_pairs, 'vocab', split_axis=1, concat_axis=0, tiled=T...  9.72 us
    all_to_all x1, starting transfers between devices, body(): lax.all_to_all(tiled_pairs, 'dp', split_axis=1, concat_axis=0, tiled=True)  9 us
  transfers between devices with their start and end apart: 11, of which 6 were waited for; matrix products, arithmetic and copies ran while one was open for 18% of the time, Pallas kernels for 0%

profile of v1, /device:TPU:1, one launch (start us, length us, event | category | flops | bytes accessed | tf_op | source)
XLA Modules:
  0.0 238.9 jit_solution(17557561283690275125)
XLA Ops:
  8.0 0.7 and_select_fusion.3
  8.7 0.7 fusion.18
  9.4 0.7 compare_and_fusion
  10.0 0.6 reduce-window.6
  11.0 0.7 add_select_fusion
  11.8 0.6 tile.2
  12.4 9.0 %all-to-all-start = ((bf16[256,8,2]{0,2,1:T(2,128)(2,1)}), bf16[256,8,2]{0,2,1:T(2,128)(2,1)S(1)}, u32[]{:S(2)}, u32[]{:S(2)}) async-start(bf16[256,8,2]{0,2,1:T(2,128)(2,1)} %tile.2), calls=%async_computation | async-start | bytes 16384 | tf_op jit(solution)/shard_map/all_to_all | solution.py:65
  21.4 0.8 convolution_convert_fusion
  22.3 2.0 copy.100
  24.3 14.6 %constant_dynamic-slice_fusion = (bf16[256,1,640]{2,1,0:T(2,128)(2,1)S(1)}, bf16[256,1,640]{2,1,0:T(2,128)(2,1)S(1)}, bf16[256,1,640]{2,1,0:T(2,128)(2,1)S(1)}, ...) fusion(bf16[256,8,640]{2,1,0:T(8,128)(2,1)} %bitcast.81, ...), kind=kLoop, calls=%fused_computation.51 | loop fusion | bytes 5242912 | tf_op jit(solution)/shard_map/dynamic-slice.7
  38.9 0.8 copy.118
  39.7 1.5 collective-permute-start
  41.1 0.8 copy.117
  41.9 2.1 collective-permute-start.1
  44.0 0.8 copy.116
  44.7 2.4 %collective-permute-start.2 = (bf16[256,640]{1,0:T(8,128)(2,1)}, bf16[256,640]{1,0:T(8,128)(2,1)}, u32[]{:S(2)}, u32[]{:S(2)}) collective-permute-start(bf16[256,640]{1,0:T(8,128)(2,1)} %bitcast.75), channel_id=1, source_target_pairs={{0,96},{32,128},{64,160},{96,192},{128,224},{160,0},{192,32},{224,... | collective-permute-start | bytes 983048 | tf_op jit(solution)/shard_map/ppermute | solution.py:34
  47.1 0.8 copy.115
  47.9 2.1 collective-permute-start.3
  50.0 0.8 copy.114
  50.8 2.4 %collective-permute-start.4 = (bf16[256,640]{1,0:T(8,128)(2,1)}, bf16[256,640]{1,0:T(8,128)(2,1)S(1)}, u32[]{:S(2)}, u32[]{:S(2)}) collective-permute-start(bf16[256,640]{1,0:T(8,128)(2,1)} %bitcast.73), channel_id=1, source_target_pairs={{0,160},{32,192},{64,224},{96,0},{128,32},{160,64},{192,96},{224,1... | collective-permute-start | bytes 983048 | tf_op jit(solution)/shard_map/ppermute | solution.py:34
  53.2 0.8 fusion.3
  53.9 0.8 copy.112
  54.7 0.8 copy.113
  55.5 0.8 copy.76
  56.3 9.7 %all-to-all-start.1 = ((bf16[8,256,2]{0,2,1:T(2,128)(2,1)}), bf16[8,256,2]{0,2,1:T(2,128)(2,1)S(1)}, u32[]{:S(2)}, u32[]{:S(2)}) async-start(bf16[8,256,2]{0,2,1:T(2,128)(2,1)} %copy.76), calls=%async_computation.1 | async-start | bytes 262144 | tf_op jit(solution)/shard_map/all_to_all | solution.py:71
  66.1 3.4 %collective-permute-start.5 = (bf16[256,640]{1,0:T(8,128)(2,1)}, bf16[256,640]{1,0:T(8,128)(2,1)S(1)}, u32[]{:S(2)}, u32[]{:S(2)}) collective-permute-start(bf16[256,640]{1,0:T(8,128)(2,1)} %bitcast.86), channel_id=1, source_target_pairs={{0,192},{32,224},{64,0},{96,32},{128,64},{160,96},{192,128},{224,1... | collective-permute-start | bytes 983048 | tf_op jit(solution)/shard_map/ppermute | solution.py:34
  69.4 1.7 bitcast_dynamic-update-slice_fusion.6
  71.2 1.2 collective-permute-start.6
  72.3 1.7 bitcast_dynamic-update-slice_fusion.5
  74.1 3.7 %collective-permute-done.2 = bf16[256,640]{1,0:T(8,128)(2,1)} collective-permute-done((bf16[256,640]{1,0:T(8,128)(2,1)}, bf16[256,640]{1,0:T(8,128)(2,1)}, u32[]{:S(2)}, u32[]{:S(2)}) %collective-permute-start.2) | collective-permute-done | bytes 327712 | tf_op jit(solution)/shard_map/ppermute | solution.py:34
  77.8 1.7 bitcast_dynamic-update-slice_fusion.4
  79.5 14.5 %collective-permute-done.3 = bf16[256,640]{1,0:T(8,128)(2,1)S(1)} collective-permute-done((bf16[256,640]{1,0:T(8,128)(2,1)}, bf16[256,640]{1,0:T(8,128)(2,1)S(1)}, u32[]{:S(2)}, u32[]{:S(2)}) %collective-permute-start.3) | collective-permute-done | bytes 327712 | tf_op jit(solution)/shard_map/ppermute | solution.py:34
  94.0 0.8 bitcast_dynamic-update-slice_fusion.3
  94.8 0.8 bitcast_dynamic-update-slice_fusion.2
  95.5 7.5 %collective-permute-done.5 = bf16[256,640]{1,0:T(8,128)(2,1)S(1)} collective-permute-done((bf16[256,640]{1,0:T(8,128)(2,1)}, bf16[256,640]{1,0:T(8,128)(2,1)S(1)}, u32[]{:S(2)}, u32[]{:S(2)}) %collective-permute-start.5) | collective-permute-done | bytes 327712 | tf_op jit(solution)/shard_map/ppermute | solution.py:34
  103.0 0.8 bitcast_dynamic-update-slice_fusion.1
  103.7 4.1 %collective-permute-done.6 = bf16[256,640]{1,0:T(8,128)(2,1)S(1)} collective-permute-done((bf16[256,640]{1,0:T(8,128)(2,1)}, bf16[256,640]{1,0:T(8,128)(2,1)S(1)}, u32[]{:S(2)}, u32[]{:S(2)}) %collective-permute-start.6) | collective-permute-done | bytes 327712 | tf_op jit(solution)/shard_map/ppermute | solution.py:34
  107.8 0.8 bitcast_dynamic-update-slice_fusion
  108.6 4.1 %gather_fusion = bf16[8,256,640]{2,1,0:T(8,128)(2,1)} fusion(bf16[8,256,640]{2,1,0:T(8,128)(2,1)} %bitcast_dynamic-update-slice_fusion, s32[1024]{0:T(1024)S(1)} %pad_clamp_fusion), kind=kCustom, calls=%fused_computation | custom fusion | bytes 5242912 | tf_op jit(solution)/shard_map/gather | solution.py:35
  112.7 4.7 %copy.87 = bf16[8,256,640]{2,0,1:T(8,128)(2,1)} copy(bf16[8,256,640]{2,1,0:T(8,128)(2,1)} %gather_fusion) | data formatting | bytes 5242880 | tf_op jit(solution)/shard_map/gather | solution.py:35
  117.4 8.6 %all-to-all-start.2 = ((bf16[8,256,640]{2,0,1:T(8,128)(2,1)}), bf16[8,256,640]{2,0,1:T(8,128)(2,1)}, u32[]{:S(2)}, u32[]{:S(2)}) async-start(bf16[8,256,640]{2,0,1:T(8,128)(2,1)} %copy.87), calls=%async_computation.2 | async-start | bytes 5242880 | tf_op jit(solution)/shard_map/all_to_all | solution.py:70
  126.1 0.2 reshape.232
  126.7 33.3 %all-to-all-done.2 = bf16[8,256,640]{2,0,1:T(8,128)(2,1)} async-done(((bf16[8,256,640]{2,0,1:T(8,128)(2,1)}), bf16[8,256,640]{2,0,1:T(8,128)(2,1)}, u32[]{:S(2)}, u32[]{:S(2)}) %all-to-all-start.2) | async-done | bytes 2621472 | tf_op jit(solution)/shard_map/all_to_all | solution.py:70
  160.0 2.4 copy.89
  162.5 0.4 copy-done.3
  162.9 4.7 %fusion.14 = (bf16[512,640]{1,0:T(8,128)(2,1)}, f32[512,640]{1,0:T(8,128)}, f32[512,640]{1,0:T(8,128)}, f32[512,640]{1,0:T(8,128)}) fusion(f32[512,640]{1,0:T(8,128)S(1)} %copy-done.1, f32[512,640]{1,0:T(8,128)S(1)} %copy-done.2, f32[512,640]{1,0:T(8,128)S(1)} %copy-done.3, bf16[2048,640]{1,0:T(8,128)(2,1)S(1)} %bitcast.83, f32[2048]{0:T(1024)S(1)} %bitcast.89), kind=kOutput, calls=%fused_computation.74 | convolution fusion | flops 1347813376 | bytes 11149312 | tf_op jit(solution)/shard_map/dot_general | solution.py:77
  167.6 59.3 %all-gather.2.cloned.1.call-done = bf16[512,5120]{1,0:T(8,128)(2,1)} async-done(((bf16[512,640]{1,0:T(8,128)(2,1)}), bf16[512,5120]{1,0:T(8,128)(2,1)}) %all-gather.2.cloned.1.call-update) | async-done | bytes 5242896 | tf_op jit(solution)/shard_map/all_gather | solution.py:82
  226.9 5.2 %copy.128 = bf16[512,5120]{1,0:T(8,128)(2,1)} copy(bf16[512,5120]{1,0:T(8,128)(2,1)} %all-gather.2.cloned.1.call-done) | data formatting | bytes 10485760
  (28 shorter events, 1.1 us)
Async XLA Ops:
  7.2 14.3 %copy-start = (bf16[256,5120]{1,0:T(8,128)(2,1)S(1)}, bf16[256,5120]{1,0:T(8,128)(2,1)}, u32[]{:S(2)}) copy-start(bf16[256,5120]{1,0:T(8,128)(2,1)} %param.8) | copy-start | bytes 7864324
  12.4 43.1 %all-to-all-start = ((bf16[256,8,2]{0,2,1:T(2,128)(2,1)}), bf16[256,8,2]{0,2,1:T(2,128)(2,1)S(1)}, u32[]{:S(2)}, u32[]{:S(2)}) async-start(bf16[256,8,2]{0,2,1:T(2,128)(2,1)} %tile.2), calls=%async_computation | async-start | bytes 16384 | tf_op jit(solution)/shard_map/all_to_all | solution.py:65
  39.7 26.4 %collective-permute-start = (bf16[256,640]{1,0:T(8,128)(2,1)}, bf16[256,640]{1,0:T(8,128)(2,1)}, u32[]{:S(2)}, u32[]{:S(2)}) collective-permute-start(bf16[256,640]{1,0:T(8,128)(2,1)} %bitcast.77), channel_id=1, source_target_pairs={{0,32},{32,64},{64,96},{96,128},{128,160},{160,192},{192,224},{224... | collective-permute-start | bytes 983048 | tf_op jit(solution)/shard_map/ppermute | solution.py:34
  41.9 29.3 %collective-permute-start.1 = (bf16[256,640]{1,0:T(8,128)(2,1)}, bf16[256,640]{1,0:T(8,128)(2,1)}, u32[]{:S(2)}, u32[]{:S(2)}) collective-permute-start(bf16[256,640]{1,0:T(8,128)(2,1)} %bitcast.76), channel_id=1, source_target_pairs={{0,64},{32,96},{64,128},{96,160},{128,192},{160,224},{192,0},{224,... | collective-permute-start | bytes 983048 | tf_op jit(solution)/shard_map/ppermute | solution.py:34
  44.7 33.0 %collective-permute-start.2 = (bf16[256,640]{1,0:T(8,128)(2,1)}, bf16[256,640]{1,0:T(8,128)(2,1)}, u32[]{:S(2)}, u32[]{:S(2)}) collective-permute-start(bf16[256,640]{1,0:T(8,128)(2,1)} %bitcast.75), channel_id=1, source_target_pairs={{0,96},{32,128},{64,160},{96,192},{128,224},{160,0},{192,32},{224,... | collective-permute-start | bytes 983048 | tf_op jit(solution)/shard_map/ppermute | solution.py:34
  47.9 46.1 %collective-permute-start.3 = (bf16[256,640]{1,0:T(8,128)(2,1)}, bf16[256,640]{1,0:T(8,128)(2,1)S(1)}, u32[]{:S(2)}, u32[]{:S(2)}) collective-permute-start(bf16[256,640]{1,0:T(8,128)(2,1)} %bitcast.74), channel_id=1, source_target_pairs={{0,128},{32,160},{64,192},{96,224},{128,0},{160,32},{192,64},{224,... | collective-permute-start | bytes 983048 | tf_op jit(solution)/shard_map/ppermute | solution.py:34
  50.8 44.0 %collective-permute-start.4 = (bf16[256,640]{1,0:T(8,128)(2,1)}, bf16[256,640]{1,0:T(8,128)(2,1)S(1)}, u32[]{:S(2)}, u32[]{:S(2)}) collective-permute-start(bf16[256,640]{1,0:T(8,128)(2,1)} %bitcast.73), channel_id=1, source_target_pairs={{0,160},{32,192},{64,224},{96,0},{128,32},{160,64},{192,96},{224,1... | collective-permute-start | bytes 983048 | tf_op jit(solution)/shard_map/ppermute | solution.py:34
  56.3 61.1 %all-to-all-start.1 = ((bf16[8,256,2]{0,2,1:T(2,128)(2,1)}), bf16[8,256,2]{0,2,1:T(2,128)(2,1)S(1)}, u32[]{:S(2)}, u32[]{:S(2)}) async-start(bf16[8,256,2]{0,2,1:T(2,128)(2,1)} %copy.76), calls=%async_computation.1 | async-start | bytes 262144 | tf_op jit(solution)/shard_map/all_to_all | solution.py:71
  66.1 36.9 %collective-permute-start.5 = (bf16[256,640]{1,0:T(8,128)(2,1)}, bf16[256,640]{1,0:T(8,128)(2,1)S(1)}, u32[]{:S(2)}, u32[]{:S(2)}) collective-permute-start(bf16[256,640]{1,0:T(8,128)(2,1)} %bitcast.86), channel_id=1, source_target_pairs={{0,192},{32,224},{64,0},{96,32},{128,64},{160,96},{192,128},{224,1... | collective-permute-start | bytes 983048 | tf_op jit(solution)/shard_map/ppermute | solution.py:34
  71.2 36.7 %collective-permute-start.6 = (bf16[256,640]{1,0:T(8,128)(2,1)}, bf16[256,640]{1,0:T(8,128)(2,1)S(1)}, u32[]{:S(2)}, u32[]{:S(2)}) collective-permute-start(bf16[256,640]{1,0:T(8,128)(2,1)} %bitcast.85), channel_id=1, source_target_pairs={{0,224},{32,0},{64,32},{96,64},{128,96},{160,128},{192,160},{224,1... | collective-permute-start | bytes 983048 | tf_op jit(solution)/shard_map/ppermute | solution.py:34
  117.4 42.6 %all-to-all-start.2 = ((bf16[8,256,640]{2,0,1:T(8,128)(2,1)}), bf16[8,256,640]{2,0,1:T(8,128)(2,1)}, u32[]{:S(2)}, u32[]{:S(2)}) async-start(bf16[8,256,640]{2,0,1:T(8,128)(2,1)} %copy.87), calls=%async_computation.2 | async-start | bytes 5242880 | tf_op jit(solution)/shard_map/all_to_all | solution.py:70
  126.0 100.9 %all-gather.2.cloned.1.call-start = ((), (), s32[]{:S(2)}) async-start(), calls=%async_computation.3 | async-start | bytes 5898240 | tf_op jit(solution)/shard_map/all_gather | solution.py:82
  160.0 2.4 copy-start.1
  160.0 2.5 %copy-start.2 = (f32[512,640]{1,0:T(8,128)S(1)}, f32[512,640]{1,0:T(8,128)}, u32[]{:S(2)}) copy-start(f32[512,640]{1,0:T(8,128)} %param.10) | copy-start | bytes 3932164
  160.0 2.9 %copy-start.3 = (f32[512,640]{1,0:T(8,128)S(1)}, f32[512,640]{1,0:T(8,128)}, u32[]{:S(2)}) copy-start(f32[512,640]{1,0:T(8,128)} %param.11) | copy-start | bytes 3932164
Sparse Core Ops, SparseCore 0:
  167.7 59.1 all-gather.1
